TPU v7x, 8 devices: a whole 2x2x1 slice. The times are simulated.
8 devices in a mesh: model: 4 (over z, y, x), data: 2 (over core).
Axes of the slice: x: 2, y: 2, z: 1, core: 2. Of those that a mesh axis runs over, the one named last changes fastest.
Arguments:
- grad_qkv: float32 [2, 12, 512, 1536], P('data', None, None, 'model')
- weight_qkv: float32 [12, 512, 1536], P(None, 'data', 'model')
- moment1_qkv: float32 [12, 512, 1536], P(None, 'data', 'model')
- moment2_qkv: float32 [12, 512, 1536], P(None, 'data', 'model')
- grad_proj: float32 [2, 12, 512, 512], P('data', None, 'model')
- weight_proj: float32 [12, 512, 512], P(None, ('model', 'data'))
- moment1_proj: float32 [12, 512, 512], P(None, ('model', 'data'))
- moment2_proj: float32 [12, 512, 512], P(None, ('model', 'data'))
- grad_fcin: float32 [2, 12, 512, 2048], P('data', None, None, 'model')
- weight_fcin: float32 [12, 512, 2048], P(None, 'data', 'model')
- moment1_fcin: float32 [12, 512, 2048], P(None, 'data', 'model')
- moment2_fcin: float32 [12, 512, 2048], P(None, 'data', 'model')
- grad_fcout: float32 [2, 12, 2048, 512], P('data', None, 'model')
- weight_fcout: float32 [12, 2048, 512], P(None, ('model', 'data'))
- moment1_fcout: float32 [12, 2048, 512], P(None, ('model', 'data'))
- moment2_fcout: float32 [12, 2048, 512], P(None, ('model', 'data'))
Outputs:
- output 1: bfloat16 [12, 512, 1536], P(None, None, 'model')
- output 2: bfloat16 [12, 512, 512], P(None, 'model')
- output 3: bfloat16 [12, 512, 2048], P(None, None, 'model')
- output 4: bfloat16 [12, 2048, 512], P(None, 'model')
- output 5: float32 [12, 512, 1536], P(None, 'data', 'model')
- output 6: float32 [12, 512, 512], P(None, ('model', 'data'))
- output 7: float32 [12, 512, 2048], P(None, 'data', 'model')
- output 8: float32 [12, 2048, 512], P(None, ('model', 'data'))
- output 9: float32 [12, 512, 1536], P(None, 'data', 'model')
- output 10: float32 [12, 512, 512], P(None, ('model', 'data'))
- output 11: float32 [12, 512, 2048], P(None, 'data', 'model')
- output 12: float32 [12, 2048, 512], P(None, ('model', 'data'))
- output 13: float32 [12, 512, 1536], P(None, 'data', 'model')
- output 14: float32 [12, 512, 512], P(None, ('model', 'data'))
- output 15: float32 [12, 512, 2048], P(None, 'data', 'model')
- output 16: float32 [12, 2048, 512], P(None, ('model', 'data'))
All inputs are finite; a program needn't handle non-finite values.
Results may differ from a plain program's by a relative error of at most 0.001.
Values are sent between devices in bfloat16 or wider.
A program may use at most 1 GiB of HBM per device.

v0:
```python
import jax
import jax.numpy as jnp
from jax import lax
from jax.sharding import PartitionSpec as P

LEARN_RATE = 0.08
BETA_ONE = 0.9
BETA_TWO = 0.999
ADAM_EPS = 1e-6
DECAY_RATE = 0.01
MAX_NORM = 1.0
STEP_COUNT = 100
COLUMN_SPLIT = (True, False, True, False)


def grad_spec(col_split):
    return P("data", None, None, "model") if col_split else P("data", None, "model", None)


def state_spec(col_split):
    return P(None, "data", "model") if col_split else P(None, ("model", "data"), None)


def replica_spec(col_split):
    return P(None, None, "model") if col_split else P(None, "model", None)


def adam_direction(grad_mean, weight, moment1, moment2, clip_coef):
    clipped = clip_coef * grad_mean
    new_first = BETA_ONE * moment1 + (1.0 - BETA_ONE) * clipped
    new_second = BETA_TWO * moment2 + (1.0 - BETA_TWO) * clipped * clipped
    first_hat = new_first / (1.0 - BETA_ONE ** STEP_COUNT)
    second_hat = new_second / (1.0 - BETA_TWO ** STEP_COUNT)
    update = first_hat / (jnp.sqrt(second_hat) + ADAM_EPS) + DECAY_RATE * weight
    return update, new_first, new_second


def solution(mesh):
    group_size = mesh.shape["data"]
    in_specs = []
    for col_split in COLUMN_SPLIT:
        in_specs.extend([grad_spec(col_split), state_spec(col_split), state_spec(col_split), state_spec(col_split)])
    out_specs = tuple([replica_spec(col_split) for col_split in COLUMN_SPLIT] + [state_spec(col_split) for col_split in COLUMN_SPLIT] * 3)

    def device_step(*arrays):
        kind_count = len(COLUMN_SPLIT)
        grad_means = []
        for kind_idx in range(kind_count):
            sent_grad = arrays[4 * kind_idx].astype(jnp.bfloat16)
            received = lax.all_to_all(sent_grad, "data", 2, 0, tiled=True)
            grad_means.append(jnp.sum(received, axis=0, dtype=jnp.float32) / group_size)
        local_sq = sum(jnp.sum(grad_mean * grad_mean) for grad_mean in grad_means)
        total_norm = jnp.sqrt(lax.psum(local_sq, ("model", "data")))
        clip_coef = jnp.minimum(1.0, MAX_NORM / total_norm)
        replicas, weights, firsts, seconds = [], [], [], []
        for kind_idx in range(kind_count):
            weight = arrays[4 * kind_idx + 1]
            update, new_first, new_second = adam_direction(grad_means[kind_idx], weight, arrays[4 * kind_idx + 2], arrays[4 * kind_idx + 3], clip_coef)
            sq_pair = jnp.stack([jnp.sum(weight * weight, axis=(1, 2)), jnp.sum(update * update, axis=(1, 2))])
            norm_pair = jnp.sqrt(lax.psum(sq_pair, ("model", "data")))
            trust_ratio = (norm_pair[0] / norm_pair[1])[:, None, None]
            new_weight = weight - LEARN_RATE * trust_ratio * update
            replicas.append(lax.all_gather(new_weight.astype(jnp.bfloat16), "data", axis=1, tiled=True))
            weights.append(new_weight)
            firsts.append(new_first)
            seconds.append(new_second)
        return tuple(replicas + weights + firsts + seconds)

    return jax.shard_map(device_step, mesh=mesh, in_specs=tuple(in_specs), out_specs=out_specs, check_vma=False)
```

profile of v0, /device:TPU:0, one launch (start us, length us, event | category | flops | bytes accessed | tf_op | source)
XLA Modules:
  0.0 305.5 jit_solution(7244588762709680788)
XLA Ops:
  7.2 4.3 %convert_element_type.56 = bf16[1,12,512,384]{3,2,1,0:T(8,128)(2,1)S(1)} convert(f32[1,12,512,384]{3,2,1,0:T(8,128)} %param.16) | non-fusion elementwise | flops 2359296 | bytes 14155776 | tf_op jit(solution)/shard_map/convert_element_type | solution.py:49
  11.5 5.8 %copy.108 = bf16[1,12,512,384]{3,1,0,2:T(8,128)(2,1)} copy(bf16[1,12,512,384]{3,2,1,0:T(8,128)(2,1)S(1)} %convert_element_type.56) | data formatting | bytes 9437184 | tf_op jit(solution)/shard_map/convert_element_type | solution.py:49
  17.3 6.6 %all-to-all-start = ((bf16[1,12,512,384]{3,1,0,2:T(8,128)(2,1)}), bf16[1,12,512,384]{3,1,0,2:T(8,128)(2,1)}, u32[]{:S(2)}, u32[]{:S(2)}) async-start(bf16[1,12,512,384]{3,1,0,2:T(8,128)(2,1)} %copy.108), calls=%async_computation | async-start | bytes 12582912 | tf_op jit(solution)/shard_map/all_to_all | solution.py:50
  23.8 0.2 convert_element_type.59
  24.1 2.2 copy.109
  26.3 3.5 %all-to-all-done = bf16[1,12,512,384]{3,1,0,2:T(8,128)(2,1)} async-done(((bf16[1,12,512,384]{3,1,0,2:T(8,128)(2,1)}), bf16[1,12,512,384]{3,1,0,2:T(8,128)(2,1)}, u32[]{:S(2)}, u32[]{:S(2)}) %all-to-all-start) | async-done | bytes 4718624 | tf_op jit(solution)/shard_map/all_to_all | solution.py:50
  29.8 5.1 %all-to-all-start.1 = ((bf16[1,12,128,512]{3,1,0,2:T(8,128)(2,1)}), bf16[1,12,128,512]{3,1,0,2:T(8,128)(2,1)}, u32[]{:S(2)}, u32[]{:S(2)}) async-start(bf16[1,12,128,512]{3,1,0,2:T(8,128)(2,1)} %copy.109), calls=%async_computation.1 | async-start | bytes 4194304 | tf_op jit(solution)/shard_map/all_to_all | solution.py:50
  34.9 4.9 %convert_reduce_fusion.2 = f32[12,256,384]{2,0,1:T(8,128)S(1)} fusion(bf16[12,2,256,384]{3,0,2,1:T(8,128)(2,1)} %bitcast.16), kind=kLoop, calls=%fused_computation.2 | loop fusion | flops 3538944 | bytes 9437184 | tf_op jit(solution)/shard_map/reduce_sum | solution.py:51
  39.8 0.0 copy-start
  39.8 2.7 copy-done
  42.5 2.2 multiply_reduce_fusion.6
  44.7 5.4 %convert_element_type.62 = bf16[1,12,512,512]{3,2,1,0:T(8,128)(2,1)S(1)} convert(f32[1,12,512,512]{3,2,1,0:T(8,128)} %param.24) | non-fusion elementwise | flops 3145728 | bytes 18874368 | tf_op jit(solution)/shard_map/convert_element_type | solution.py:49
  50.2 7.2 %copy.110 = bf16[1,12,512,512]{3,1,0,2:T(8,128)(2,1)} copy(bf16[1,12,512,512]{3,2,1,0:T(8,128)(2,1)S(1)} %convert_element_type.62) | data formatting | bytes 12582912 | tf_op jit(solution)/shard_map/convert_element_type | solution.py:49
  57.4 0.0 all-to-all-done.1
  57.4 7.4 %all-to-all-start.2 = ((bf16[1,12,512,512]{3,1,0,2:T(8,128)(2,1)}), bf16[1,12,512,512]{3,1,0,2:T(8,128)(2,1)}, u32[]{:S(2)}, u32[]{:S(2)}) async-start(bf16[1,12,512,512]{3,1,0,2:T(8,128)(2,1)} %copy.110), calls=%async_computation.2 | async-start | bytes 16777216 | tf_op jit(solution)/shard_map/all_to_all | solution.py:50
  64.8 2.3 convert_reduce_fusion.3
  67.2 0.0 copy-start.1
  67.2 1.3 copy-done.1
  68.5 1.1 multiply_reduce_fusion.9
  69.6 5.4 %convert_element_type.65 = bf16[1,12,512,512]{3,2,1,0:T(8,128)(2,1)S(1)} convert(f32[1,12,512,512]{3,2,1,0:T(8,128)} %param.28) | non-fusion elementwise | flops 3145728 | bytes 18874368 | tf_op jit(solution)/shard_map/convert_element_type | solution.py:49
  75.1 7.2 %copy.111 = bf16[1,12,512,512]{3,1,0,2:T(8,128)(2,1)} copy(bf16[1,12,512,512]{3,2,1,0:T(8,128)(2,1)S(1)} %convert_element_type.65) | data formatting | bytes 12582912 | tf_op jit(solution)/shard_map/convert_element_type | solution.py:49
  82.3 0.0 all-to-all-done.2
  82.3 7.0 %all-to-all-start.3 = ((bf16[1,12,512,512]{3,1,0,2:T(8,128)(2,1)}), bf16[1,12,512,512]{3,1,0,2:T(8,128)(2,1)}, u32[]{:S(2)}, u32[]{:S(2)}) async-start(bf16[1,12,512,512]{3,1,0,2:T(8,128)(2,1)} %copy.111), calls=%async_computation.3 | async-start | bytes 16777216 | tf_op jit(solution)/shard_map/all_to_all | solution.py:50
  89.3 0.2 all-gather.7.cloned.1.call-start
  89.5 9.9 %convert_reduce_fusion.1 = f32[12,256,512]{2,0,1:T(8,128)} fusion(bf16[12,2,256,512]{3,0,2,1:T(8,128)(2,1)} %bitcast.18), kind=kLoop, calls=%fused_computation.1 | loop fusion | flops 4718592 | bytes 12582912 | tf_op jit(solution)/shard_map/reduce_sum | solution.py:51
  99.3 6.1 %multiply_reduce_fusion.1 = f32[]{:T(128)} fusion(f32[12,256,512]{2,0,1:T(8,128)} %convert_reduce_fusion.1), kind=kLoop, calls=%fused_computation.6 | loop fusion | flops 4718591 | bytes 6291460 | tf_op jit(solution)/shard_map/reduce_sum | solution.py:52
  105.5 0.0 all-to-all-done.3
  105.5 9.9 %convert_reduce_fusion = f32[12,256,512]{2,0,1:T(8,128)} fusion(bf16[12,2,256,512]{3,0,2,1:T(8,128)(2,1)} %bitcast.19), kind=kLoop, calls=%fused_computation | loop fusion | flops 4718592 | bytes 12582912 | tf_op jit(solution)/shard_map/reduce_sum | solution.py:51
  115.3 6.3 %multiply_reduce_fusion = f32[]{:T(128)} fusion(f32[12,256,512]{2,0,1:T(8,128)} %convert_reduce_fusion), kind=kLoop, calls=%fused_computation.5 | loop fusion | flops 4718591 | bytes 6291460 | tf_op jit(solution)/shard_map/reduce_sum | solution.py:52
  124.2 24.9 %psum.35 = f32[]{:T(128)} all-reduce(f32[]{:T(128)S(6)} %add.75), channel_id=1, replica_groups=mesh['model'=4,'data'=2] {'model','data'}, use_global_device_ids=true, to_apply=%region_9.0 | all-reduce | flops 1 | bytes 8 | tf_op jit(solution)/shard_map/psum | solution.py:53
  149.8 0.0 slice-start.1
  149.8 32.9 %multiply_reduce_fusion.3 = (f32[12]{0:T(128)S(1)}, f32[12]{0:T(128)S(1)}, f32[12,256,512]{2,1,0:T(8,128)}, f32[12,256,512]{2,1,0:T(8,128)}, f32[12]{0:T(128)S(1...) fusion(f32[12,256,512]{2,1,0:T(8,128)} %param.29, f32[]{:T(128)S(6)} %mul.245, ...), kind=kLoop, calls=%fused_computation.16 | loop fusion | flops 56623056 | bytes 75497664 | tf_op jit(solution)/shard_map/reduce_sum | solution.py:59
  182.7 0.0 slice-done
  182.7 0.0 slice-done.1
  182.8 0.0 copy-start.2
  182.8 0.0 copy-start.3
  182.8 0.0 copy-start.8
  182.8 0.0 copy-start.9
  182.8 11.7 %multiply_reduce_fusion.8 = (f32[12]{0:T(128)S(1)}, f32[12]{0:T(128)S(1)}, f32[12,256,384]{2,1,0:T(8,128)}, f32[12,256,384]{2,1,0:T(8,128)}) fusion(f32[12,256,384]{2,1,0:T(8,128)} %param.17, f32[]{:T(128)S(6)} %mul.245, f32[12,256,384]{2,0,1:T(8,128)S(1)} %bitcast.25, f32[12,256,384]{2,1,0:T(8,128)} %param.18, f32[12,256,384]{2,1,0:T(8,128)} %param.19), kind=kLoop, calls=%fused_computation.29 | loop fusion | flops 21233640 | bytes 28311652 | tf_op jit(solution)/shard_map/reduce_sum | solution.py:59
  194.5 0.0 copy-done.8
  194.6 0.0 copy-start.4
  194.6 3.3 %multiply_reduce_fusion.11 = (f32[12]{0:T(128)S(1)}, f32[12]{0:T(128)S(1)}, f32[12,64,512]{2,1,0:T(8,128)S(1)}, f32[12,64,512]{2,1,0:T(8,128)}) fusion(f32[12,64,512]{2,1,0:T(8,128)S(1)} %copy-done.3, f32[]{:T(128)S(6)} %mul.245, f32[12,64,512]{2,0,1:T(8,128)S(1)} %copy-done.2, f32[12,64,512]{2,1,0:T(8,128)S(1)} %copy-done.8, f32[12,64,512]{2,1,0:T(8,128)S(1)} %copy-done.9), kind=kLoop, calls=%fused_computation.39 | loop fusion | flops 7077864 | bytes 9437284 | tf_op jit(solution)/shard_map/reduce_sum | solution.py:59
  197.8 23.5 %all-reduce = (f32[2,12]{1,0:T(2,128)S(1)}, f32[2,12]{1,0:T(2,128)S(1)}, f32[2,12]{1,0:T(2,128)S(1)}, f32[2,12]{1,0:T(2,128)S(1)}) all-reduce(f32[2,12]{1,0:T(2,128)S(1)} %get-tuple-element.80, f32[2,12]{1,0:T(2,128)S(1)} %get-tuple-element.81, ...), channel_id=1, replica_groups=mesh['model'=4,'data'=2] {'model','data'}, use_global_device_ids=true, to_apply=%region_11.0 | all-reduce | flops 96 | bytes 768 | tf_op jit(solution)/shard_map/psum | solution.py:60
  221.4 3.7 %fusion.6 = (bf16[12,64,512]{2,1,0:T(8,128)(2,1)}, f32[12,64,512]{2,1,0:T(8,128)}) fusion(f32[12,64,512]{2,1,0:T(8,128)S(1)} %copy-done.4, f32[12,64,512]{2,1,0:T(8,128)} %get-tuple-element.111, f32[12,64,512]{2,1,0:T(8,128)S(1)} %get-tuple-element.107, f32[12]{0:T(128)S(1)} %multiply_bitcast_fusion.2), kind=kLoop, calls=%fused_computation.54 | loop fusion | flops 3538944 | bytes 7077936 | tf_op jit(solution)/shard_map/convert_element_type | solution.py:63
  225.0 0.0 all-gather.7.cloned.1.call-update
  225.1 0.0 all-gather.5.cloned.1.call-start
  225.1 8.2 %fusion.7 = (bf16[12,256,384]{2,1,0:T(8,128)(2,1)}, f32[12,256,384]{2,1,0:T(8,128)}) fusion(f32[12,256,384]{2,1,0:T(8,128)} %param.17, f32[12,256,384]{2,1,0:T(8,128)} %get-tuple-element.110, f32[12,256,384]{2,1,0:T(8,128)} %get-tuple-element.106, f32[12]{0:T(128)S(1)} %multiply_bitcast_fusion.3), kind=kLoop, calls=%fused_computation.55 | loop fusion | flops 10616832 | bytes 21233712 | tf_op jit(solution)/shard_map/convert_element_type | solution.py:63
  233.4 0.0 all-gather.5.cloned.1.call-update
  233.4 0.0 all-gather.11.cloned.1.call-start
  233.5 10.4 %fusion.4 = (bf16[12,256,512]{2,1,0:T(8,128)(2,1)}, f32[12,256,512]{2,1,0:T(8,128)}) fusion(f32[12,256,512]{2,1,0:T(8,128)} %param.29, f32[12,256,512]{2,1,0:T(8,128)} %get-tuple-element.113, f32[12,256,512]{2,1,0:T(8,128)} %get-tuple-element.109, f32[12]{0:T(128)S(1)} %multiply_bitcast_fusion), kind=kLoop, calls=%fused_computation.52 | loop fusion | flops 14155776 | bytes 28311600 | tf_op jit(solution)/shard_map/convert_element_type | solution.py:63
  243.8 0.0 all-gather.11.cloned.1.call-update
  243.8 0.0 all-gather.9.cloned.1.call-start
  243.9 10.4 %fusion.5 = (bf16[12,256,512]{2,1,0:T(8,128)(2,1)}, f32[12,256,512]{2,1,0:T(8,128)}) fusion(f32[12,256,512]{2,1,0:T(8,128)} %param.25, f32[12,256,512]{2,1,0:T(8,128)} %get-tuple-element.112, f32[12,256,512]{2,1,0:T(8,128)} %get-tuple-element.108, f32[12]{0:T(128)S(1)} %multiply_bitcast_fusion.1), kind=kLoop, calls=%fused_computation.53 | loop fusion | flops 14155776 | bytes 28311600 | tf_op jit(solution)/shard_map/convert_element_type | solution.py:63
  254.3 0.0 all-gather.9.cloned.1.call-update
  254.3 0.0 all-gather.7.cloned.1.call-done
  254.3 0.0 all-gather.5.cloned.1.call-done
  254.4 12.9 %all-gather.11.cloned.1.call-done = bf16[12,512,512]{2,1,0:T(8,128)(2,1)} async-done(((bf16[12,256,512]{2,1,0:T(8,128)(2,1)}), bf16[12,512,512]{2,1,0:T(8,128)(2,1)}) %all-gather.11.cloned.1.call-update) | async-done | bytes 6291472 | tf_op jit(solution)/shard_map/all_gather | solution.py:63
  267.2 17.8 %all-gather.9.cloned.1.call-done = bf16[12,512,512]{2,1,0:T(8,128)(2,1)} async-done(((bf16[12,256,512]{2,1,0:T(8,128)(2,1)}), bf16[12,512,512]{2,1,0:T(8,128)(2,1)}) %all-gather.9.cloned.1.call-update) | async-done | bytes 6291472 | tf_op jit(solution)/shard_map/all_gather | solution.py:63
  285.0 5.2 %copy.148 = bf16[12,512,384]{2,1,0:T(8,128)(2,1)} copy(bf16[12,512,384]{2,1,0:T(8,128)(2,1)} %all-gather.5.cloned.1.call-done) | data formatting | bytes 9437184
  290.2 1.1 copy.149
  291.3 3.2 %copy.150 = bf16[12,512,512]{2,1,0:T(8,128)(2,1)} copy(bf16[12,512,512]{2,1,0:T(8,128)(2,1)S(1)} %bitcast.29) | data formatting | bytes 12582912
  294.5 0.0 slice-done.2
  294.5 1.5 slice-done.3
  296.0 2.7 copy.151
  (31 shorter events, 0.1 us)
Async XLA Ops:
  17.3 6.6 %copy-start.6 = (f32[1,12,128,512]{3,2,1,0:T(8,128)S(1)}, f32[1,12,128,512]{3,2,1,0:T(8,128)}, u32[]{:S(2)}) copy-start(f32[1,12,128,512]{3,2,1,0:T(8,128)} %param.20) | copy-start | bytes 9437188
  17.3 12.5 %all-to-all-start = ((bf16[1,12,512,384]{3,1,0,2:T(8,128)(2,1)}), bf16[1,12,512,384]{3,1,0,2:T(8,128)(2,1)}, u32[]{:S(2)}, u32[]{:S(2)}) async-start(bf16[1,12,512,384]{3,1,0,2:T(8,128)(2,1)} %copy.108), calls=%async_computation | async-start | bytes 12582912 | tf_op jit(solution)/shard_map/all_to_all | solution.py:50
  29.8 27.6 %all-to-all-start.1 = ((bf16[1,12,128,512]{3,1,0,2:T(8,128)(2,1)}), bf16[1,12,128,512]{3,1,0,2:T(8,128)(2,1)}, u32[]{:S(2)}, u32[]{:S(2)}) async-start(bf16[1,12,128,512]{3,1,0,2:T(8,128)(2,1)} %copy.109), calls=%async_computation.1 | async-start | bytes 4194304 | tf_op jit(solution)/shard_map/all_to_all | solution.py:50
  39.8 2.7 copy-start
  57.4 24.9 %all-to-all-start.2 = ((bf16[1,12,512,512]{3,1,0,2:T(8,128)(2,1)}), bf16[1,12,512,512]{3,1,0,2:T(8,128)(2,1)}, u32[]{:S(2)}, u32[]{:S(2)}) async-start(bf16[1,12,512,512]{3,1,0,2:T(8,128)(2,1)} %copy.110), calls=%async_computation.2 | async-start | bytes 16777216 | tf_op jit(solution)/shard_map/all_to_all | solution.py:50
  67.2 1.3 copy-start.1
  82.3 23.2 %all-to-all-start.3 = ((bf16[1,12,512,512]{3,1,0,2:T(8,128)(2,1)}), bf16[1,12,512,512]{3,1,0,2:T(8,128)(2,1)}, u32[]{:S(2)}, u32[]{:S(2)}) async-start(bf16[1,12,512,512]{3,1,0,2:T(8,128)(2,1)} %copy.111), calls=%async_computation.3 | async-start | bytes 16777216 | tf_op jit(solution)/shard_map/all_to_all | solution.py:50
  89.3 165.1 %all-gather.7.cloned.1.call-start = ((), (), s32[]{:S(2)}) async-start(), calls=%async_computation.5 | async-start | bytes 2359296 | tf_op jit(solution)/shard_map/all_gather | solution.py:63
  115.3 67.4 %slice-start = ((s8[6291456]{0:T(1024)(128)(4,1)}), s8[2097152]{0:T(1024)(128)(4,1)S(1)}, s32[]{:S(2)}) async-start(s8[6291456]{0:T(1024)(128)(4,1)} %bitcast.24), calls=%async_computation.8 | async-start | bytes 4194304
  149.8 32.9 %slice-start.1 = ((s8[6291456]{0:T(1024)(128)(4,1)}), s8[4194304]{0:T(1024)(128)(4,1)S(1)}, s32[]{:S(2)}) async-start(s8[6291456]{0:T(1024)(128)(4,1)} %bitcast.24), calls=%async_computation.9 | async-start | bytes 8388608
  182.8 11.8 %copy-start.2 = (f32[12,64,512]{2,0,1:T(8,128)S(1)}, f32[12,64,512]{2,0,1:T(8,128)}, u32[]{:S(2)}) copy-start(f32[12,64,512]{2,0,1:T(8,128)} %copy-done.1) | copy-start | bytes 4718596
  182.8 11.8 %copy-start.3 = (f32[12,64,512]{2,1,0:T(8,128)S(1)}, f32[12,64,512]{2,1,0:T(8,128)}, u32[]{:S(2)}) copy-start(f32[12,64,512]{2,1,0:T(8,128)} %param.21) | copy-start | bytes 4718596
  182.8 11.8 %copy-start.8 = (f32[12,64,512]{2,1,0:T(8,128)S(1)}, f32[12,64,512]{2,1,0:T(8,128)}, u32[]{:S(2)}) copy-start(f32[12,64,512]{2,1,0:T(8,128)} %param.22) | copy-start | bytes 4718596
  182.8 11.8 %copy-start.9 = (f32[12,64,512]{2,1,0:T(8,128)S(1)}, f32[12,64,512]{2,1,0:T(8,128)}, u32[]{:S(2)}) copy-start(f32[12,64,512]{2,1,0:T(8,128)} %param.23) | copy-start | bytes 4718596
  194.6 26.8 %copy-start.4 = (f32[12,64,512]{2,1,0:T(8,128)S(1)}, f32[12,64,512]{2,1,0:T(8,128)}, u32[]{:S(2)}) copy-start(f32[12,64,512]{2,1,0:T(8,128)} %param.21) | copy-start | bytes 4718596
  197.8 35.5 %copy-start.5 = (f32[12,64,512]{2,1,0:T(8,128)}, f32[12,64,512]{2,1,0:T(8,128)S(1)}, u32[]{:S(2)}) copy-start(f32[12,64,512]{2,1,0:T(8,128)S(1)} %get-tuple-element.107) | copy-start | bytes 4718596
  225.1 29.3 %all-gather.5.cloned.1.call-start = ((), (), s32[]{:S(2)}) async-start(), calls=%async_computation.4 | async-start | bytes 7077888 | tf_op jit(solution)/shard_map/all_gather | solution.py:63
  233.4 33.8 %all-gather.11.cloned.1.call-start = ((), (), s32[]{:S(2)}) async-start(), calls=%async_computation.7 | async-start | bytes 9437184 | tf_op jit(solution)/shard_map/all_gather | solution.py:63
  243.8 41.2 %all-gather.9.cloned.1.call-start = ((), (), s32[]{:S(2)}) async-start(), calls=%async_computation.6 | async-start | bytes 9437184 | tf_op jit(solution)/shard_map/all_gather | solution.py:63
  254.3 35.8 %copy-start.7 = (bf16[12,128,512]{2,1,0:T(8,128)(2,1)S(1)}, bf16[12,128,512]{2,1,0:T(8,128)(2,1)}, u32[]{:S(2)}) copy-start(bf16[12,128,512]{2,1,0:T(8,128)(2,1)} %all-gather.7.cloned.1.call-done) | copy-start | bytes 4718596
  285.0 6.3 %slice-start.4 = ((s8[6291456]{0:T(1024)(128)(4,1)}), s8[4194304]{0:T(1024)(128)(4,1)S(1)}, s32[]{:S(2)}) async-start(s8[6291456]{0:T(1024)(128)(4,1)} %bitcast.28), calls=%async_computation.12 | async-start | bytes 8388608
  285.0 6.3 %slice-start.5 = ((s8[6291456]{0:T(1024)(128)(4,1)}), s8[2097152]{0:T(1024)(128)(4,1)S(1)}, s32[]{:S(2)}) async-start(s8[6291456]{0:T(1024)(128)(4,1)} %bitcast.28), calls=%async_computation.13 | async-start | bytes 4194304
  290.2 4.4 %slice-start.2 = ((s8[6291456]{0:T(1024)(128)(4,1)}), s8[4194304]{0:T(1024)(128)(4,1)S(1)}, s32[]{:S(2)}) async-start(s8[6291456]{0:T(1024)(128)(4,1)} %bitcast.26), calls=%async_computation.10 | async-start | bytes 8388608
  291.3 4.7 %slice-start.3 = ((s8[6291456]{0:T(1024)(128)(4,1)}), s8[2097152]{0:T(1024)(128)(4,1)S(1)}, s32[]{:S(2)}) async-start(s8[6291456]{0:T(1024)(128)(4,1)} %bitcast.26), calls=%async_computation.11 | async-start | bytes 4194304
Sparse Core Ops, SparseCore 0:
  225.2 8.6 all-gather.6
  236.0 13.2 all-gather.4
  251.4 15.7 all-gather.10
  269.2 15.7 all-gather.8
where the time goes:
time: 311 us; the launch traced here: 306 us
  other arithmetic  139 us (45%)
  blocking collectives  48.4 us (16%)
  local copies, waits for them, and re-layouts  40.2 us (13%)
  waiting for transfers between devices  34.3 us (11%)
  starting transfers between devices  26.4 us (8%)
  between operations  17.6 us (6%)
    reduce_sum x3, other arithmetic, device_step(): jnp.sum(weight * weight, axis=(1, 2))  47.8 us
    convert_element_type x4, other arithmetic, device_step(): new_weight.astype(jnp.bfloat16)  32.6 us
    all_gather x4, waiting for transfers between devices, device_step(): lax.all_gather(new_weight.astype(jnp.bfloat16), 'data', axis=1, tiled=True)  30.7 us
    reduce_sum x4, other arithmetic, device_step(): grad_means.append(jnp.sum(received, axis=0, dtype=jnp.float32) / group_size)  26.9 us
    all_to_all x4, starting transfers between devices, device_step(): received = lax.all_to_all(sent_grad, 'data', 2, 0, tiled=True)  26.1 us
    psum x1, blocking collectives, device_step(): total_norm = jnp.sqrt(lax.psum(local_sq, ('model', 'data')))  24.9 us
    psum x1, blocking collectives, device_step(): norm_pair = jnp.sqrt(lax.psum(sq_pair, ('model', 'data')))  23.5 us
    convert_element_type x4, local copies, waits for them, and re-layouts, device_step(): sent_grad = arrays[4 * kind_idx].astype(jnp.bfloat16)  22.4 us
  transfers between devices with their start and end apart: 8, of which 3 were waited for; matrix products, arithmetic and copies ran while one was open for 27% of the time, Pallas kernels for 0%

commit v1 on v0

v1 whole, which is shorter than its diff:
```python
import functools

import jax
import jax.numpy as jnp
from jax import lax
from jax.experimental import pallas as pl
from jax.experimental.pallas import tpu as pltpu
from jax.sharding import PartitionSpec as P

LEARN_RATE = 0.08
BETA_ONE = 0.9
BETA_TWO = 0.999
ADAM_EPS = 1e-6
DECAY_RATE = 0.01
MAX_NORM = 1.0
STEP_COUNT = 100
COLUMN_SPLIT = (True, False, True, False)
ORDER = (2, 3, 0, 1)
MESH_ID = pl.DeviceIdType.MESH
SCOPED_BYTES = 25 * 2**19

STAGE_SLOTS = 4
SEND_SLOTS = 4
COMBINE_LAG = 3
STATE_SLOTS = 12
STATE_AHEAD = 6


def grad_spec(col_split):
    return P("data", None, None, "model") if col_split else P("data", None, "model", None)


def state_spec(col_split):
    return P(None, "data", "model") if col_split else P(None, ("model", "data"), None)


def replica_spec(col_split):
    return P(None, None, "model") if col_split else P(None, "model", None)


def at_offset(pos, idx, off, layers, count, action):
    target = idx + off
    if off == 0:
        action(pos, idx)
    elif off > 0:
        pl.when(target < layers)(lambda: action(pos, target))
        if pos + 1 < count:
            pl.when(target >= layers)(lambda: action(pos + 1, target - layers))
    else:
        pl.when(target >= 0)(lambda: action(pos, target))
        if pos > 0:
            pl.when(target < 0)(lambda: action(pos - 1, target + layers))


def fold_lanes(acc):
    return functools.reduce(jnp.add, [acc[:, lo:lo + 128] for lo in range(0, acc.shape[1], 128)])


class Resident:
    def __init__(self, ref, layers, shapes):
        self.ref, self.shapes = ref, shapes
        full = max(rows for rows, _ in shapes)
        self.packed = [full // rows for rows, _ in shapes]
        self.base, total = [], 0
        for packed in self.packed:
            self.base.append(total)
            total += -(-layers // packed)
        self.slots = total

    def spot(self, pos, layer):
        packed = self.packed[pos]
        if packed == 1:
            return self.base[pos] + layer, 0
        rows = self.shapes[pos][0]
        return self.base[pos] + layer // packed, pl.multiple_of(lax.rem(layer, packed) * rows, rows)

    def block(self, which, pos, layer):
        rows, cols = self.shapes[pos]
        slot, row = self.spot(pos, layer)
        return self.ref.at[which, slot, pl.ds(row, rows), pl.ds(0, cols)]


def other_devices(model_size, data_size):
    return [(dm, dd) for dm in range(model_size) for dd in range(data_size) if (dm, dd) != (0, 0)]


class Peers:
    def __init__(self, model_size, data_size):
        self.model_size, self.data_size = model_size, data_size
        self.me_m, self.me_d = lax.axis_index("model"), lax.axis_index("data")
        self.me = self.me_m * data_size + self.me_d
        self.offsets = other_devices(model_size, data_size)

    def there(self, off):
        return lax.rem(self.me_m + off[0], self.model_size), lax.rem(self.me_d + off[1], self.data_size)

    def back(self, off):
        from_m = lax.rem(self.me_m + self.model_size - off[0], self.model_size)
        from_d = lax.rem(self.me_d + self.data_size - off[1], self.data_size)
        return from_m * self.data_size + from_d

    def arrive(self):
        barrier = pltpu.get_barrier_semaphore()
        for off in self.offsets:
            to_m, to_d = self.there(off)
            pl.semaphore_signal(barrier, inc=1, device_id=(to_m, to_d), device_id_type=MESH_ID)

    def await_all(self):
        pl.semaphore_wait(pltpu.get_barrier_semaphore(), len(self.offsets))

    def copies(self, slots, send_sem, recv_sem):
        out = []
        for num, off in enumerate(self.offsets):
            to_m, to_d = self.there(off)
            out.append(pltpu.make_async_remote_copy(
                src_ref=slots.at[self.me], dst_ref=slots.at[self.me], send_sem=send_sem.at[num],
                recv_sem=recv_sem.at[self.me], device_id=(to_m, to_d), device_id_type=MESH_ID))
        return out

    def wait_copies(self, copies, slots, send_sem, recv_sem):
        for num, off in enumerate(self.offsets):
            src = self.back(off)
            copies[num].wait_send()
            to_m, to_d = self.there(off)
            pltpu.make_async_remote_copy(
                src_ref=slots.at[src], dst_ref=slots.at[src], send_sem=send_sem.at[num],
                recv_sem=recv_sem.at[src], device_id=(to_m, to_d), device_id_type=MESH_ID).wait_recv()


def grad_kernel(dims, g0, g1, g2, g3, w0, w1, w2, w3, held_ref, coef_ref,
                r0, r1, r2, r3, stage, outbox, acc_ref, slots, other_sem, own_sem, w_sem, send_sem, recv_sem, tile_send, tile_recv):
    layers, shapes, model_size, data_size = dims
    grads, weights = [(g0, g1, g2, g3)[k] for k in ORDER], [(w0, w1, w2, w3)[k] for k in ORDER]
    inbox, shapes = [(r0, r1, r2, r3)[k] for k in ORDER], [shapes[k] for k in ORDER]
    count = len(ORDER)
    held = Resident(held_ref, layers, shapes)
    peers = Peers(model_size, data_size)
    mine, theirs = peers.me_d, 1 - peers.me_d
    peers.arrive()

    def number(pos, layer):
        return pos * layers + layer

    def rows_of(pos, who):
        return pl.ds(pl.multiple_of(who * shapes[pos][0], shapes[pos][0]), shapes[pos][0])

    def load_other(pos, layer):
        rows, cols = shapes[pos]
        slot = lax.rem(number(pos, layer), STAGE_SLOTS)
        return pltpu.make_async_copy(grads[pos].at[0, layer, rows_of(pos, theirs), :], stage.at[slot, pl.ds(0, rows), pl.ds(0, cols)], other_sem.at[slot])

    def load_own(pos, layer):
        return pltpu.make_async_copy(grads[pos].at[0, layer, rows_of(pos, mine), :], held.block(0, pos, layer), own_sem.at[number(pos, layer)])

    def load_weight(pos, layer):
        return pltpu.make_async_copy(weights[pos].at[layer], held.block(1, pos, layer), w_sem.at[number(pos, layer)])

    def send(pos, layer):
        rows, cols = shapes[pos]
        slot = lax.rem(number(pos, layer), SEND_SLOTS)
        return pltpu.make_async_remote_copy(
            src_ref=outbox.at[slot, pl.ds(0, rows), pl.ds(0, cols)], dst_ref=inbox[pos].at[layer], send_sem=send_sem.at[slot],
            recv_sem=recv_sem.at[number(pos, layer)], device_id=(peers.me_m, theirs), device_id_type=MESH_ID)

    def pack(pos, layer):
        rows, cols = shapes[pos]
        num = number(pos, layer)
        slot, box = lax.rem(num, STAGE_SLOTS), lax.rem(num, SEND_SLOTS)
        load_other(pos, layer).wait()

        def step(t, _):
            at = pl.ds(pl.multiple_of(t * 32, 32), 32)
            outbox[box, at, pl.ds(0, cols)] = stage[slot, at, pl.ds(0, cols)].astype(jnp.bfloat16)
            return 0

        lax.fori_loop(0, rows // 32, step, 0, unroll=2)

    def combine(pos, layer):
        rows, cols = shapes[pos]
        load_own(pos, layer).wait()
        send(pos, layer).wait_recv()
        block, row = held.spot(pos, layer)
        wide = pl.ds(0, cols)

        def step(t, acc):
            at = pl.ds(pl.multiple_of(t * 16, 16), 16)
            there = pl.ds(pl.multiple_of(row + t * 16, 16), 16)
            own = held_ref[0, block, there, wide].astype(jnp.bfloat16).astype(jnp.float32)
            mean = (own + inbox[pos][layer, at, :].astype(jnp.float32)) * (1.0 / data_size)
            held_ref[0, block, there, wide] = mean
            sq = mean * mean
            return acc + sq[:8] + sq[8:]

        acc = lax.fori_loop(0, rows // 16, step, jnp.zeros((8, cols), jnp.float32), unroll=2)
        acc_ref[...] += fold_lanes(acc)

    acc_ref[...] = jnp.zeros_like(acc_ref)
    for layer in range(STAGE_SLOTS):
        load_other(0, layer).start()
        load_own(0, layer).start()
    for layer in range(2):
        load_weight(0, layer).start()
    for pos in range(count):
        def body(layer, _, pos=pos):
            if pos == 0:
                pl.when(layer >= SEND_SLOTS)(lambda: send(pos, layer - SEND_SLOTS).wait_send())
            else:
                at_offset(pos, layer, -SEND_SLOTS, layers, count, lambda p, l: send(p, l).wait_send())
            pack(pos, layer)
            if pos == 0:
                pl.when(layer == 0)(peers.await_all)
            at_offset(pos, layer, -1, layers, count, lambda p, l: send(p, l).start())

            def ahead(p, l):
                load_other(p, l).start()
                load_own(p, l).start()

            at_offset(pos, layer, STAGE_SLOTS, layers, count, ahead)
            at_offset(pos, layer, 2, layers, count, lambda p, l: load_weight(p, l).start())
            at_offset(pos, layer, -COMBINE_LAG, layers, count, combine)
            return 0

        lax.fori_loop(0, layers, body, 0)
    last = count - 1
    send(last, layers - 1).start()
    for layer in range(layers - COMBINE_LAG, layers):
        combine(last, layer)
    for layer in range(layers - SEND_SLOTS, layers):
        send(last, layer).wait_send()

    slots[peers.me] = acc_ref[...]
    copies = peers.copies(slots, tile_send, tile_recv)
    for copy in copies:
        copy.start()
    for pos in range(count):
        def drain(layer, _, pos=pos):
            load_weight(pos, layer).wait()
            return 0

        lax.fori_loop(0, layers, drain, 0)
    peers.wait_copies(copies, slots, tile_send, tile_recv)
    total = functools.reduce(jnp.add, [slots[n] for n in range(model_size * data_size)])
    total = jnp.sum(jnp.sum(total, axis=1, keepdims=True), axis=0, keepdims=True)
    coef_ref[...] = jnp.broadcast_to(jnp.minimum(1.0, MAX_NORM / jnp.sqrt(total)), coef_ref.shape)


def adam_kernel(dims, *refs):
    layers, shapes = dims
    count = len(ORDER)
    coef_ref = refs[0]
    m_in, v_in, held_ref, m_out, v_out = refs[2:6], refs[6:10], refs[10], refs[11:15], refs[15:19]
    usq_ref, wsq_ref, ring, load_sem, store_sem = refs[19:]
    pick = lambda group: [group[k] for k in ORDER]
    m_in, v_in, m_out, v_out, shapes = map(pick, (m_in, v_in, m_out, v_out, shapes))
    held = Resident(held_ref, layers, shapes)
    coef = jnp.max(coef_ref[...])

    def number(pos, layer):
        return pos * layers + layer

    def window(pos, slot, which):
        rows, cols = shapes[pos]
        return ring.at[slot, which, pl.ds(0, rows), pl.ds(0, cols)]

    def loads(pos, layer):
        slot = lax.rem(number(pos, layer), STATE_SLOTS)
        return [pltpu.make_async_copy(src[pos].at[layer], window(pos, slot, which), load_sem.at[slot, which]) for which, src in enumerate((m_in, v_in))]

    def stores(pos, layer):
        slot = lax.rem(number(pos, layer), STATE_SLOTS)
        return [pltpu.make_async_copy(window(pos, slot, which), dst[pos].at[layer], store_sem.at[slot, which]) for which, dst in enumerate((m_out, v_out))]

    def start_loads(pos, layer):
        for copy in loads(pos, layer):
            copy.start()

    def wait_stores(pos, layer):
        for copy in stores(pos, layer):
            copy.wait()

    def compute(pos, layer):
        rows, cols = shapes[pos]
        num = number(pos, layer)
        slot = lax.rem(num, STATE_SLOTS)
        block, row = held.spot(pos, layer)

        def step(t, accs):
            at, wide = pl.ds(pl.multiple_of(t * 8, 8), 8), pl.ds(0, cols)
            there = pl.ds(pl.multiple_of(row + t * 8, 8), 8)
            clipped = coef * held_ref[0, block, there, wide]
            weight = held_ref[1, block, there, wide]
            first = BETA_ONE * ring[slot, 0, at, wide] + (1.0 - BETA_ONE) * clipped
            second = BETA_TWO * ring[slot, 1, at, wide] + (1.0 - BETA_TWO) * clipped * clipped
            ring[slot, 0, at, wide] = first
            ring[slot, 1, at, wide] = second
            first_hat = first * (1.0 / (1.0 - BETA_ONE ** STEP_COUNT))
            second_hat = second * (1.0 / (1.0 - BETA_TWO ** STEP_COUNT))
            update = first_hat / (jnp.sqrt(second_hat) + ADAM_EPS) + DECAY_RATE * weight
            held_ref[0, block, there, wide] = update
            return accs[0] + update * update, accs[1] + weight * weight

        zero = jnp.zeros((8, cols), jnp.float32)
        usq, wsq = lax.fori_loop(0, rows // 8, step, (zero, zero), unroll=2)
        usq_ref[num] = fold_lanes(usq)
        wsq_ref[num] = fold_lanes(wsq)

    for layer in range(STATE_AHEAD):
        start_loads(0, layer)
    for pos in range(count):
        def body(layer, _, pos=pos):
            at_offset(pos, layer, STATE_AHEAD - STATE_SLOTS, layers, count, wait_stores)
            at_offset(pos, layer, STATE_AHEAD, layers, count, start_loads)
            for copy in loads(pos, layer):
                copy.wait()
            compute(pos, layer)
            for copy in stores(pos, layer):
                copy.start()
            return 0

        lax.fori_loop(0, layers, body, 0)
    for layer in range(layers - STATE_SLOTS + STATE_AHEAD, layers):
        wait_stores(count - 1, layer)


def weight_kernel(dims, usq_ref, wsq_ref, _, held_ref, r0, r1, r2, r3, outbox, slots, tile_send, tile_recv, send_sem, recv_sem):
    layers, shapes, model_size, data_size = dims
    count = len(ORDER)
    inbox, shapes = [(r0, r1, r2, r3)[k] for k in ORDER], [shapes[k] for k in ORDER]
    held = Resident(held_ref, layers, shapes)
    peers = Peers(model_size, data_size)
    peers.arrive()

    def number(pos, layer):
        return pos * layers + layer

    def send(pos, layer):
        rows, cols = shapes[pos]
        block, row = held.spot(pos, layer)
        return pltpu.make_async_remote_copy(
            src_ref=outbox.at[block, pl.ds(row, rows), pl.ds(0, cols)], dst_ref=inbox[pos].at[layer], send_sem=send_sem.at[number(pos, layer)],
            recv_sem=recv_sem.at[number(pos, layer)], device_id=(peers.me_m, 1 - peers.me_d), device_id_type=MESH_ID)

    def by_lane(ref):
        part = jnp.sum(ref[...], axis=1)
        part = jnp.concatenate([part, jnp.zeros((128 - part.shape[0], 128), jnp.float32)], axis=0)
        return jnp.sum(part.T, axis=0, keepdims=True)

    row = lax.broadcasted_iota(jnp.int32, (8, 128), 0)
    lane = lax.broadcasted_iota(jnp.int32, (8, 128), 1)
    slots[peers.me] = jnp.where(row == 0, by_lane(usq_ref), by_lane(wsq_ref))
    peers.await_all()
    copies = peers.copies(slots, tile_send, tile_recv)
    for copy in copies:
        copy.start()
    peers.wait_copies(copies, slots, tile_send, tile_recv)
    total = functools.reduce(jnp.add, [slots[n] for n in range(model_size * data_size)])
    root = jnp.sqrt(total)
    live = (row == 1) & (lane < count * layers)
    rates = jnp.where(live, LEARN_RATE * (root / jnp.where(lane < count * layers, root[0:1], 1.0)), 0.0)

    for pos in range(count):
        rows, cols = shapes[pos]

        def body(layer, _, pos=pos, rows=rows, cols=cols):
            num = number(pos, layer)
            rate = jnp.sum(jnp.where(lane == num, rates, 0.0))
            block, row = held.spot(pos, layer)
            wide = pl.ds(0, cols)

            def step(t, _):
                there = pl.ds(pl.multiple_of(row + t * 16, 16), 16)
                new = held_ref[1, block, there, wide] - rate * held_ref[0, block, there, wide]
                held_ref[1, block, there, wide] = new
                outbox[block, there, wide] = new.astype(jnp.bfloat16)
                return 0

            lax.fori_loop(0, rows // 16, step, 0, unroll=2)
            at_offset(pos, layer, -1, layers, count, lambda p, l: send(p, l).start())
            return 0

        lax.fori_loop(0, layers, body, 0)
    send(count - 1, layers - 1).start()
    for pos in range(count):
        def drain(layer, _, pos=pos):
            send(pos, layer).wait()
            return 0

        lax.fori_loop(0, layers, drain, 0)


def write_kernel(dims, held_ref, i0, i1, i2, i3, w0, w1, w2, w3, r0, r1, r2, r3, outbox, weight_sem, inbox_sem, own_sem):
    layers, shapes = dims
    count = len(ORDER)
    pick = lambda group: [group[k] for k in ORDER]
    inbox, weights, replicas, shapes = map(pick, ((i0, i1, i2, i3), (w0, w1, w2, w3), (r0, r1, r2, r3), shapes))
    held = Resident(held_ref, layers, shapes)
    me_d = lax.axis_index("data")

    def rows_of(pos, who):
        return pl.ds(pl.multiple_of(who * shapes[pos][0], shapes[pos][0]), shapes[pos][0])

    def weight_copy(pos, layer):
        return pltpu.make_async_copy(held.block(1, pos, layer), weights[pos].at[layer], weight_sem.at[pos * layers + layer])

    def inbox_copy(pos, layer):
        return pltpu.make_async_copy(inbox[pos].at[layer], replicas[pos].at[layer, rows_of(pos, 1 - me_d), :], inbox_sem.at[pos * layers + layer])

    def own_copy(pos, layer):
        rows, cols = shapes[pos]
        slot = lax.rem(pos * layers + layer, SEND_SLOTS)
        return pltpu.make_async_copy(outbox.at[slot, pl.ds(0, rows), pl.ds(0, cols)], replicas[pos].at[layer, rows_of(pos, me_d), :], own_sem.at[slot])

    for pos in range(count):
        rows, cols = shapes[pos]

        def body(layer, _, pos=pos, rows=rows, cols=cols):
            weight_copy(pos, layer).start()
            inbox_copy(pos, layer).start()
            if pos == 0:
                pl.when(layer >= SEND_SLOTS)(lambda: own_copy(pos, layer - SEND_SLOTS).wait())
            else:
                at_offset(pos, layer, -SEND_SLOTS, layers, count, lambda p, l: own_copy(p, l).wait())
            slot = lax.rem(pos * layers + layer, SEND_SLOTS)
            block, row = held.spot(pos, layer)
            wide = pl.ds(0, cols)

            def step(t, _):
                at, there = pl.ds(pl.multiple_of(t * 32, 32), 32), pl.ds(pl.multiple_of(row + t * 32, 32), 32)
                outbox[slot, at, wide] = held_ref[1, block, there, wide].astype(jnp.bfloat16)
                return 0

            lax.fori_loop(0, rows // 32, step, 0, unroll=2)
            own_copy(pos, layer).start()
            return 0

        lax.fori_loop(0, layers, body, 0)
    for layer in range(layers - SEND_SLOTS, layers):
        own_copy(count - 1, layer).wait()
    for pos in range(count):
        def drain(layer, _, pos=pos):
            weight_copy(pos, layer).wait()
            inbox_copy(pos, layer).wait()
            return 0

        lax.fori_loop(0, layers, drain, 0)


def solution(mesh):
    model_size, data_size = mesh.shape["model"], mesh.shape["data"]
    in_specs = []
    for col_split in COLUMN_SPLIT:
        in_specs.extend([grad_spec(col_split), state_spec(col_split), state_spec(col_split), state_spec(col_split)])
    out_specs = tuple([replica_spec(col_split) for col_split in COLUMN_SPLIT] + [state_spec(col_split) for col_split in COLUMN_SPLIT] * 3)
    hbm, vmem = pl.BlockSpec(memory_space=pltpu.HBM), pl.BlockSpec(memory_space=pltpu.VMEM)

    def in_hbm(values):
        return [pltpu.with_memory_space_constraint(value, pltpu.HBM) for value in values]

    def in_vmem(values):
        return [pltpu.with_memory_space_constraint(value, pltpu.VMEM) for value in values]

    def device_step(*arrays):
        grads, weights, firsts, seconds = (list(arrays[n::4]) for n in range(4))
        kinds = len(COLUMN_SPLIT)
        layers = weights[0].shape[0]
        units = kinds * layers
        shapes = [weight.shape[1:] for weight in weights]
        rows_max, cols_max = max(s[0] for s in shapes), max(s[1] for s in shapes)
        held_type = pltpu.VMEM((2, Resident(None, layers, [shapes[k] for k in ORDER]).slots, rows_max, cols_max), jnp.float32)
        state_hbm = [jax.ShapeDtypeStruct(weight.shape, jnp.float32) for weight in weights]
        sums = pltpu.VMEM((units, 8, 128), jnp.float32)
        devices = model_size * data_size
        dma = pltpu.SemaphoreType.DMA

        held, coef = pl.pallas_call(
            functools.partial(grad_kernel, (layers, shapes, model_size, data_size)),
            out_shape=[held_type, pltpu.VMEM((8, 128), jnp.float32)],
            in_specs=[hbm] * 8, out_specs=[vmem] * 2,
            scratch_shapes=[pltpu.VMEM(weight.shape, jnp.bfloat16) for weight in weights] + [
                pltpu.VMEM((STAGE_SLOTS, rows_max, cols_max), jnp.float32), pltpu.VMEM((SEND_SLOTS, rows_max, cols_max), jnp.bfloat16),
                pltpu.VMEM((8, 128), jnp.float32), pltpu.VMEM((devices, 8, 128), jnp.float32),
                dma((STAGE_SLOTS,)), dma((units,)), dma((units,)), dma((SEND_SLOTS,)), dma((units,)), dma((devices - 1,)), dma((devices,))],
            compiler_params=pltpu.CompilerParams(collective_id=0, has_side_effects=True, vmem_limit_bytes=SCOPED_BYTES),
            name="grad_mean",
        )(*in_hbm(grads + weights))

        outs = pl.pallas_call(
            functools.partial(adam_kernel, (layers, shapes)),
            out_shape=[held_type] + state_hbm + state_hbm + [sums, sums],
            in_specs=[vmem] * 2 + [hbm] * 8, out_specs=[vmem] + [hbm] * 8 + [vmem] * 2,
            input_output_aliases={1: 0},
            scratch_shapes=[pltpu.VMEM((STATE_SLOTS, 2, rows_max, cols_max), jnp.float32), dma((STATE_SLOTS, 2)), dma((STATE_SLOTS, 2))],
            compiler_params=pltpu.CompilerParams(vmem_limit_bytes=SCOPED_BYTES),
            name="adam",
        )(*in_vmem([coef, held]), *in_hbm(firsts + seconds))
        held, new_firsts, new_seconds, usq, wsq = outs[0], outs[1:5], outs[5:9], outs[9], outs[10]

        outs = pl.pallas_call(
            functools.partial(weight_kernel, (layers, shapes, model_size, data_size)),
            out_shape=[held_type] + [pltpu.VMEM(weight.shape, jnp.bfloat16) for weight in weights],
            in_specs=[vmem] * 3, out_specs=[vmem] * 5,
            input_output_aliases={2: 0},
            scratch_shapes=[pltpu.VMEM(held_type.shape[1:], jnp.bfloat16), pltpu.VMEM((devices, 8, 128), jnp.float32),
                            dma((devices - 1,)), dma((devices,)), dma((units,)), dma((units,))],
            compiler_params=pltpu.CompilerParams(collective_id=1, has_side_effects=True, vmem_limit_bytes=SCOPED_BYTES),
            name="new_weight",
        )(*in_vmem([usq, wsq, held]))

        outs = pl.pallas_call(
            functools.partial(write_kernel, (layers, shapes)),
            out_shape=state_hbm + [jax.ShapeDtypeStruct((layers, data_size * rows, cols), jnp.bfloat16) for rows, cols in shapes],
            in_specs=[vmem] * 5, out_specs=[hbm] * 8,
            scratch_shapes=[pltpu.VMEM((SEND_SLOTS, rows_max, cols_max), jnp.bfloat16), dma((units,)), dma((units,)), dma((SEND_SLOTS,))],
            compiler_params=pltpu.CompilerParams(vmem_limit_bytes=SCOPED_BYTES),
            name="write_out",
        )(*in_vmem(outs))
        return tuple(outs[4:]) + tuple(outs[:4]) + tuple(new_firsts) + tuple(new_seconds)

    return jax.shard_map(device_step, mesh=mesh, in_specs=tuple(in_specs), out_specs=out_specs, check_vma=False)
```

time: 311 us -> 105 us (0.34); the launches traced: 306 us -> 105 us
  other arithmetic: 139 us -> 0 us
  Pallas kernels: 0 us -> 104 us
  blocking collectives: 48.4 us -> 0 us
  local copies, waits for them, and re-layouts: 40.2 us -> 0 us
  waiting for transfers between devices: 34.3 us -> 0 us
  starting transfers between devices: 26.4 us -> 0 us
  between operations: 17.6 us -> 0.67 us
    pallas_call x0 -> x4, Pallas kernels: none -> 104 us  [the longest x1 37.1 us: device_step(): pl.pallas_call(functools.partial(adam_kernel, (layers, shapes)), out_shap...]
    reduce_sum x11 -> x0, other arithmetic: 90.5 us -> none  [the longest x3 47.8 us: device_step(): jnp.sum(weight * weight, axis=(1, 2))]
    psum x2 -> x0, blocking collectives: 48.4 us -> none  [the longest x1 24.9 us: device_step(): total_norm = jnp.sqrt(lax.psum(local_sq, ('model', 'data')))]
    convert_element_type x8 -> x0, other arithmetic: 48 us -> none  [the longest x4 32.6 us: device_step(): new_weight.astype(jnp.bfloat16)]
    all_gather x4 -> x0, waiting for transfers between devices: 30.7 us -> none  [device_step(): lax.all_gather(new_weight.astype(jnp.bfloat16), 'data', axis=1, tiled=True)]
    all_to_all x4 -> x0, starting transfers between devices: 26.1 us -> none  [device_step(): received = lax.all_to_all(sent_grad, 'data', 2, 0, tiled=True)]
    convert_element_type x4 -> x0, local copies, waits for them, and re-layouts: 22.4 us -> none  [device_step(): sent_grad = arrays[4 * kind_idx].astype(jnp.bfloat16)]
    unnamed x36 -> x0, local copies, waits for them, and re-layouts: 17.8 us -> none
  transfers between devices with their start and end apart: 8 -> 0, of which waited for: 3 -> 0; matrix products, arithmetic and copies ran while one was open for 27% -> 0% of each run, Pallas kernels for 0% -> 0%
where the time goes in v1:
time: 105 us
  Pallas kernels  104 us (99%)
    pallas_call x1, Pallas kernels, device_step(): pl.pallas_call(functools.partial(adam_kernel, (layers, shapes)), out_shap...  37.1 us
    pallas_call x1, Pallas kernels, device_step(): pl.pallas_call(functools.partial(grad_kernel, (layers, shapes, model_size...  32.1 us
    pallas_call x1, Pallas kernels, device_step(): pl.pallas_call(functools.partial(weight_kernel, (layers, shapes, model_si...  20.5 us
    pallas_call x1, Pallas kernels, device_step(): pl.pallas_call(functools.partial(write_kernel, (layers, shapes)), out_sha...  14.3 us

profile of v1, /device:TPU:0, one launch (start us, length us, event | category | flops | bytes accessed | tf_op | source)
XLA Modules:
  0.0 104.6 jit_solution(6435260945046608466)
XLA Ops:
  0.6 32.1 %grad_mean.1 = (f32[2,39,256,512]{3,2,1,0:T(8,128)S(1)}, f32[8,128]{1,0:T(8,128)S(1)}) custom-call(f32[1,12,512,384]{3,2,1,0:T(8,128)} %g0.1, f32[1,12,128,512]{3,2,1,0:T(8,128)} %g1.1, f32[1,12,512,512]{3,2,1,0:T(8,128)} %g2.1, f32[1,12,512,512]{3,2,1,0:T(8,128)} %g3.1, f32[12,256,384]{2,1,0:T(8,128)} %w0.1, f32[12,64,512]{2,1,0:T(8,128)} %w1.1, ...), custom_call_target="tpu_custom_call" | custom-call | tf_op jit(solution)/shard_map/grad_mean/pallas_call | solution.py:475
  32.7 37.1 %adam.1 = (f32[2,39,256,512]{3,2,1,0:T(8,128)S(1)}, f32[12,256,384]{2,1,0:T(8,128)}, f32[12,64,512]{2,1,0:T(8,128)}, f32[12,256,512]{2,1,0:T(8,128)}, f32[12,256...) custom-call(f32[8,128]{1,0:T(8,128)S(1)} %get-tuple-element.42.refs_, ...), custom_call_target="tpu_custom_call", output_to_operand_aliasing={{0}: (1, {})} | custom-call | tf_op jit(solution)/shard_map/adam/pallas_call | solution.py:487
  69.9 20.5 %new_weight.1 = (f32[2,39,256,512]{3,2,1,0:T(8,128)S(1)}, bf16[12,256,384]{2,1,0:T(8,128)(2,1)S(1)}, bf16[12,64,512]{2,1,0:T(8,128)(2,1)S(1)}, bf16[12,256,512]{...) custom-call(f32[48,8,128]{2,1,0:T(8,128)S(1)} %get-tuple-element.44.usq_ref, ...), custom_call_target="tpu_custom_call", output_to_operand_aliasing={{0}: (2, {})} | custom-call | tf_op jit(solution)/shard_map/new_weight/pallas_call | solution.py:498
  90.3 14.3 %write_out.1 = (f32[12,256,384]{2,1,0:T(8,128)}, f32[12,64,512]{2,1,0:T(8,128)}, f32[12,256,512]{2,1,0:T(8,128)}, f32[12,256,512]{2,1,0:T(8,128)}, bf16[12,512,3...) custom-call(f32[2,39,256,512]{3,2,1,0:T(8,128)S(1)} %get-tuple-eleme, ...), custom_call_target="tpu_custom_call" | custom-call | tf_op jit(solution)/shard_map/write_out/pallas_call | solution.py:509

commit v2 on v1

--- a/solution.py
+++ b/solution.py
@@ -17,13 +17,17 @@
 COLUMN_SPLIT = (True, False, True, False)
 ORDER = (2, 3, 0, 1)
 MESH_ID = pl.DeviceIdType.MESH
-SCOPED_BYTES = 25 * 2**19
-
-STAGE_SLOTS = 4
-SEND_SLOTS = 4
-COMBINE_LAG = 3
+SCOPED_BYTES = 53 * 2**18
+
+STAGE_SLOTS = 5
+SEND_SLOTS = 6
+COMBINE_LAG = 8
+WEIGHT_AHEAD = 4
 STATE_SLOTS = 12
 STATE_AHEAD = 6
+PACK_SLOTS = 12
+STEP_ROWS = 32
+TINY = 1.1754944e-38
 
 
 def grad_spec(col_split):
@@ -52,6 +56,10 @@
             pl.when(target < 0)(lambda: action(pos - 1, target + layers))
 
 
+def fold_rows(block):
+    return functools.reduce(jnp.add, [block[lo:lo + 8] for lo in range(0, block.shape[0], 8)])
+
+
 def fold_lanes(acc):
     return functools.reduce(jnp.add, [acc[:, lo:lo + 128] for lo in range(0, acc.shape[1], 128)])
 
@@ -75,9 +83,12 @@
         return self.base[pos] + layer // packed, pl.multiple_of(lax.rem(layer, packed) * rows, rows)
 
     def block(self, which, pos, layer):
+        return self.part(self.ref.at[which], pos, layer)
+
+    def part(self, ref, pos, layer):
         rows, cols = self.shapes[pos]
         slot, row = self.spot(pos, layer)
-        return self.ref.at[which, slot, pl.ds(row, rows), pl.ds(0, cols)]
+        return ref.at[slot, pl.ds(row, rows), pl.ds(0, cols)]
 
 
 def other_devices(model_size, data_size):
@@ -183,22 +194,21 @@
         wide = pl.ds(0, cols)
 
         def step(t, acc):
-            at = pl.ds(pl.multiple_of(t * 16, 16), 16)
-            there = pl.ds(pl.multiple_of(row + t * 16, 16), 16)
+            at = pl.ds(pl.multiple_of(t * 32, 32), 32)
+            there = pl.ds(pl.multiple_of(row + t * 32, 32), 32)
             own = held_ref[0, block, there, wide].astype(jnp.bfloat16).astype(jnp.float32)
             mean = (own + inbox[pos][layer, at, :].astype(jnp.float32)) * (1.0 / data_size)
             held_ref[0, block, there, wide] = mean
-            sq = mean * mean
-            return acc + sq[:8] + sq[8:]
-
-        acc = lax.fori_loop(0, rows // 16, step, jnp.zeros((8, cols), jnp.float32), unroll=2)
+            return acc + fold_rows(mean * mean)
+
+        acc = lax.fori_loop(0, rows // 32, step, jnp.zeros((8, cols), jnp.float32))
         acc_ref[...] += fold_lanes(acc)
 
     acc_ref[...] = jnp.zeros_like(acc_ref)
     for layer in range(STAGE_SLOTS):
         load_other(0, layer).start()
         load_own(0, layer).start()
-    for layer in range(2):
+    for layer in range(WEIGHT_AHEAD):
         load_weight(0, layer).start()
     for pos in range(count):
         def body(layer, _, pos=pos):
@@ -216,15 +226,19 @@
                 load_own(p, l).start()
 
             at_offset(pos, layer, STAGE_SLOTS, layers, count, ahead)
-            at_offset(pos, layer, 2, layers, count, lambda p, l: load_weight(p, l).start())
+            at_offset(pos, layer, WEIGHT_AHEAD, layers, count, lambda p, l: load_weight(p, l).start())
             at_offset(pos, layer, -COMBINE_LAG, layers, count, combine)
             return 0
 
         lax.fori_loop(0, layers, body, 0)
     last = count - 1
     send(last, layers - 1).start()
-    for layer in range(layers - COMBINE_LAG, layers):
+
+    def finish(layer, _):
         combine(last, layer)
+        return 0
+
+    lax.fori_loop(layers - COMBINE_LAG, layers, finish, 0)
     for layer in range(layers - SEND_SLOTS, layers):
         send(last, layer).wait_send()
 
@@ -254,6 +268,9 @@
     m_in, v_in, m_out, v_out, shapes = map(pick, (m_in, v_in, m_out, v_out, shapes))
     held = Resident(held_ref, layers, shapes)
     coef = jnp.max(coef_ref[...])
+    first_scale, second_scale = (1.0 - BETA_ONE) * coef, (1.0 - BETA_TWO) ** 0.5 * coef
+    first_fix = 1.0 - BETA_ONE ** STEP_COUNT
+    root_scale, eps_scale = first_fix / (1.0 - BETA_TWO ** STEP_COUNT) ** 0.5, first_fix * ADAM_EPS
 
     def number(pos, layer):
         return pos * layers + layer
@@ -285,22 +302,21 @@
         block, row = held.spot(pos, layer)
 
         def step(t, accs):
-            at, wide = pl.ds(pl.multiple_of(t * 8, 8), 8), pl.ds(0, cols)
-            there = pl.ds(pl.multiple_of(row + t * 8, 8), 8)
-            clipped = coef * held_ref[0, block, there, wide]
-            weight = held_ref[1, block, there, wide]
-            first = BETA_ONE * ring[slot, 0, at, wide] + (1.0 - BETA_ONE) * clipped
-            second = BETA_TWO * ring[slot, 1, at, wide] + (1.0 - BETA_TWO) * clipped * clipped
+            at, wide = pl.ds(pl.multiple_of(t * STEP_ROWS, STEP_ROWS), STEP_ROWS), pl.ds(0, cols)
+            there = pl.ds(pl.multiple_of(row + t * STEP_ROWS, STEP_ROWS), STEP_ROWS)
+            mean, weight = held_ref[0, block, there, wide], held_ref[1, block, there, wide]
+            first = BETA_ONE * ring[slot, 0, at, wide] + first_scale * mean
+            scaled = second_scale * mean
+            second = BETA_TWO * ring[slot, 1, at, wide] + scaled * scaled
+            root = second * lax.rsqrt(jnp.maximum(second, TINY))
+            update = first / (root * root_scale + eps_scale) + DECAY_RATE * weight
             ring[slot, 0, at, wide] = first
             ring[slot, 1, at, wide] = second
-            first_hat = first * (1.0 / (1.0 - BETA_ONE ** STEP_COUNT))
-            second_hat = second * (1.0 / (1.0 - BETA_TWO ** STEP_COUNT))
-            update = first_hat / (jnp.sqrt(second_hat) + ADAM_EPS) + DECAY_RATE * weight
             held_ref[0, block, there, wide] = update
-            return accs[0] + update * update, accs[1] + weight * weight
+            return accs[0] + fold_rows(update * update), accs[1] + fold_rows(weight * weight)
 
         zero = jnp.zeros((8, cols), jnp.float32)
-        usq, wsq = lax.fori_loop(0, rows // 8, step, (zero, zero), unroll=2)
+        usq, wsq = lax.fori_loop(0, rows // STEP_ROWS, step, (zero, zero))
         usq_ref[num] = fold_lanes(usq)
         wsq_ref[num] = fold_lanes(wsq)
 
@@ -322,10 +338,10 @@
         wait_stores(count - 1, layer)
 
 
-def weight_kernel(dims, usq_ref, wsq_ref, _, held_ref, r0, r1, r2, r3, outbox, slots, tile_send, tile_recv, send_sem, recv_sem):
+def weight_kernel(dims, usq_ref, wsq_ref, _, held_ref, inbox, outbox, slots, tile_send, tile_recv, send_sem, recv_sem):
     layers, shapes, model_size, data_size = dims
     count = len(ORDER)
-    inbox, shapes = [(r0, r1, r2, r3)[k] for k in ORDER], [shapes[k] for k in ORDER]
+    shapes = [shapes[k] for k in ORDER]
     held = Resident(held_ref, layers, shapes)
     peers = Peers(model_size, data_size)
     peers.arrive()
@@ -334,10 +350,8 @@
         return pos * layers + layer
 
     def send(pos, layer):
-        rows, cols = shapes[pos]
-        block, row = held.spot(pos, layer)
         return pltpu.make_async_remote_copy(
-            src_ref=outbox.at[block, pl.ds(row, rows), pl.ds(0, cols)], dst_ref=inbox[pos].at[layer], send_sem=send_sem.at[number(pos, layer)],
+            src_ref=held.part(outbox, pos, layer), dst_ref=held.part(inbox, pos, layer), send_sem=send_sem.at[number(pos, layer)],
             recv_sem=recv_sem.at[number(pos, layer)], device_id=(peers.me_m, 1 - peers.me_d), device_id_type=MESH_ID)
 
     def by_lane(ref):
@@ -388,11 +402,11 @@
         lax.fori_loop(0, layers, drain, 0)
 
 
-def write_kernel(dims, held_ref, i0, i1, i2, i3, w0, w1, w2, w3, r0, r1, r2, r3, outbox, weight_sem, inbox_sem, own_sem):
+def write_kernel(dims, held_ref, inbox, w0, w1, w2, w3, r0, r1, r2, r3, outbox, weight_sem, inbox_sem, own_sem):
     layers, shapes = dims
     count = len(ORDER)
     pick = lambda group: [group[k] for k in ORDER]
-    inbox, weights, replicas, shapes = map(pick, ((i0, i1, i2, i3), (w0, w1, w2, w3), (r0, r1, r2, r3), shapes))
+    weights, replicas, shapes = map(pick, ((w0, w1, w2, w3), (r0, r1, r2, r3), shapes))
     held = Resident(held_ref, layers, shapes)
     me_d = lax.axis_index("data")
 
@@ -403,24 +417,29 @@
         return pltpu.make_async_copy(held.block(1, pos, layer), weights[pos].at[layer], weight_sem.at[pos * layers + layer])
 
     def inbox_copy(pos, layer):
-        return pltpu.make_async_copy(inbox[pos].at[layer], replicas[pos].at[layer, rows_of(pos, 1 - me_d), :], inbox_sem.at[pos * layers + layer])
+        return pltpu.make_async_copy(held.part(inbox, pos, layer), replicas[pos].at[layer, rows_of(pos, 1 - me_d), :], inbox_sem.at[pos * layers + layer])
 
     def own_copy(pos, layer):
         rows, cols = shapes[pos]
-        slot = lax.rem(pos * layers + layer, SEND_SLOTS)
+        slot = lax.rem(pos * layers + layer, PACK_SLOTS)
         return pltpu.make_async_copy(outbox.at[slot, pl.ds(0, rows), pl.ds(0, cols)], replicas[pos].at[layer, rows_of(pos, me_d), :], own_sem.at[slot])
 
     for pos in range(count):
-        rows, cols = shapes[pos]
-
-        def body(layer, _, pos=pos, rows=rows, cols=cols):
+        def issue(layer, _, pos=pos):
             weight_copy(pos, layer).start()
             inbox_copy(pos, layer).start()
+            return 0
+
+        lax.fori_loop(0, layers, issue, 0)
+    for pos in range(count):
+        rows, cols = shapes[pos]
+
+        def body(layer, _, pos=pos, rows=rows, cols=cols):
             if pos == 0:
-                pl.when(layer >= SEND_SLOTS)(lambda: own_copy(pos, layer - SEND_SLOTS).wait())
+                pl.when(layer >= PACK_SLOTS)(lambda: own_copy(pos, layer - PACK_SLOTS).wait())
             else:
-                at_offset(pos, layer, -SEND_SLOTS, layers, count, lambda p, l: own_copy(p, l).wait())
-            slot = lax.rem(pos * layers + layer, SEND_SLOTS)
+                at_offset(pos, layer, -PACK_SLOTS, layers, count, lambda p, l: own_copy(p, l).wait())
+            slot = lax.rem(pos * layers + layer, PACK_SLOTS)
             block, row = held.spot(pos, layer)
             wide = pl.ds(0, cols)
 
@@ -434,7 +453,7 @@
             return 0
 
         lax.fori_loop(0, layers, body, 0)
-    for layer in range(layers - SEND_SLOTS, layers):
+    for layer in range(layers - PACK_SLOTS, layers):
         own_copy(count - 1, layer).wait()
     for pos in range(count):
         def drain(layer, _, pos=pos):
@@ -497,8 +516,8 @@
 
         outs = pl.pallas_call(
             functools.partial(weight_kernel, (layers, shapes, model_size, data_size)),
-            out_shape=[held_type] + [pltpu.VMEM(weight.shape, jnp.bfloat16) for weight in weights],
-            in_specs=[vmem] * 3, out_specs=[vmem] * 5,
+            out_shape=[held_type, pltpu.VMEM(held_type.shape[1:], jnp.bfloat16)],
+            in_specs=[vmem] * 3, out_specs=[vmem] * 2,
             input_output_aliases={2: 0},
             scratch_shapes=[pltpu.VMEM(held_type.shape[1:], jnp.bfloat16), pltpu.VMEM((devices, 8, 128), jnp.float32),
                             dma((devices - 1,)), dma((devices,)), dma((units,)), dma((units,))],
@@ -509,8 +528,8 @@
         outs = pl.pallas_call(
             functools.partial(write_kernel, (layers, shapes)),
             out_shape=state_hbm + [jax.ShapeDtypeStruct((layers, data_size * rows, cols), jnp.bfloat16) for rows, cols in shapes],
-            in_specs=[vmem] * 5, out_specs=[hbm] * 8,
-            scratch_shapes=[pltpu.VMEM((SEND_SLOTS, rows_max, cols_max), jnp.bfloat16), dma((units,)), dma((units,)), dma((SEND_SLOTS,))],
+            in_specs=[vmem] * 2, out_specs=[hbm] * 8,
+            scratch_shapes=[pltpu.VMEM((PACK_SLOTS, rows_max, cols_max), jnp.bfloat16), dma((units,)), dma((units,)), dma((PACK_SLOTS,))],
             compiler_params=pltpu.CompilerParams(vmem_limit_bytes=SCOPED_BYTES),
             name="write_out",
         )(*in_vmem(outs))

time: 105 us -> 88.6 us (0.84)
  Pallas kernels: 104 us -> 87.7 us
    pallas_call x1, Pallas kernels: 37.1 us -> 26.2 us  [device_step(): pl.pallas_call(functools.partial(adam_kernel, (layers, shapes)), out_shap...]
    pallas_call x1, Pallas kernels: 32.1 us -> 27.2 us  [device_step(): pl.pallas_call(functools.partial(grad_kernel, (layers, shapes, model_size...]
where the time goes in v2:
time: 88.6 us; the launch traced here: 88.3 us
  Pallas kernels  87.7 us (99%)
    pallas_call x1, Pallas kernels, device_step(): pl.pallas_call(functools.partial(grad_kernel, (layers, shapes, model_size...  27.2 us
    pallas_call x1, Pallas kernels, device_step(): pl.pallas_call(functools.partial(adam_kernel, (layers, shapes)), out_shap...  26.2 us
    pallas_call x1, Pallas kernels, device_step(): pl.pallas_call(functools.partial(weight_kernel, (layers, shapes, model_si...  20.5 us
    pallas_call x1, Pallas kernels, device_step(): pl.pallas_call(functools.partial(write_kernel, (layers, shapes)), out_sha...  13.8 us

profile of v2, /device:TPU:0, one launch (start us, length us, event | category | flops | bytes accessed | tf_op | source)
XLA Modules:
  0.0 88.3 jit_solution(10346788270962013226)
XLA Ops:
  0.6 27.2 %grad_mean.1 = (f32[2,39,256,512]{3,2,1,0:T(8,128)S(1)}, f32[8,128]{1,0:T(8,128)S(1)}) custom-call(f32[1,12,512,384]{3,2,1,0:T(8,128)} %g0.1, f32[1,12,128,512]{3,2,1,0:T(8,128)} %g1.1, f32[1,12,512,512]{3,2,1,0:T(8,128)} %g2.1, f32[1,12,512,512]{3,2,1,0:T(8,128)} %g3.1, f32[12,256,384]{2,1,0:T(8,128)} %w0.1, f32[12,64,512]{2,1,0:T(8,128)} %w1.1, ...), custom_call_target="tpu_custom_call" | custom-call | tf_op jit(solution)/shard_map/grad_mean/pallas_call | solution.py:494
  27.9 26.2 %adam.1 = (f32[2,39,256,512]{3,2,1,0:T(8,128)S(1)}, f32[12,256,384]{2,1,0:T(8,128)}, f32[12,64,512]{2,1,0:T(8,128)}, f32[12,256,512]{2,1,0:T(8,128)}, f32[12,256...) custom-call(f32[8,128]{1,0:T(8,128)S(1)} %get-tuple-element.39.refs_, ...), custom_call_target="tpu_custom_call", output_to_operand_aliasing={{0}: (1, {})} | custom-call | tf_op jit(solution)/shard_map/adam/pallas_call | solution.py:506
  54.1 20.5 %new_weight.1 = (f32[2,39,256,512]{3,2,1,0:T(8,128)S(1)}, bf16[39,256,512]{2,1,0:T(8,128)(2,1)S(1)}) custom-call(f32[48,8,128]{2,1,0:T(8,128)S(1)} %get-tuple-element.41.usq_ref, f32[48,8,128]{2,1,0:T(8,128)S(1)} %get-tuple-element.42.wsq_ref, f32[2,39,256,512]{3,2,1,0:T(8,128)S(1)} %get-tuple-element.43._), custom_call_target="tpu_custom_call", output_to_operand_aliasing={{0}: (2, {})} | custom-call | tf_op jit(solution)/shard_map/new_weight/pallas_call | solution.py:517
  74.5 13.8 %write_out.1 = (f32[12,256,384]{2,1,0:T(8,128)}, f32[12,64,512]{2,1,0:T(8,128)}, f32[12,256,512]{2,1,0:T(8,128)}, f32[12,256,512]{2,1,0:T(8,128)}, bf16[12,512,3...) custom-call(f32[2,39,256,512]{3,2,1,0:T(8,128)S(1)} %get-tuple-eleme, ...), custom_call_target="tpu_custom_call" | custom-call | tf_op jit(solution)/shard_map/write_out/pallas_call | solution.py:528
